TPU v7x, 32 devices: a whole 2x2x4 slice. The times are simulated.
32 devices in a mesh: section: 4 (over y, x), tp: 8 (over z, core).
Axes of the slice: x: 2, y: 2, z: 4, core: 2. Of those that a mesh axis runs over, the one named last changes fastest.
Arguments:
- grad_in: bfloat16 [4, 128, 4096], P('section', None, 'tp'), may hold values from -6 to 6
- fresh_grads: bfloat16 [1, 128, 4096], P(None, None, 'tp'), may hold values from -6 to 6
- acc_in: float32 [4, 128, 4096], P('section', None, 'tp'), may hold values from -3 to 3
- queries: bfloat16 [4, 2, 128, 4096], P('section', None, None, 'tp'), may hold values from -4.625 to 4.625
- keys: bfloat16 [4, 2, 128, 4096], P('section', None, None, 'tp'), may hold values from -4.625 to 4.625
- values: bfloat16 [4, 2, 128, 4096], P('section', None, None, 'tp'), may hold values from -12 to 12
- query_weight: bfloat16 [4, 4096, 4096], P('section', 'tp'), may hold values from -0.09375 to 0.09375
- key_weight: bfloat16 [4, 4096, 4096], P('section', None, 'tp'), may hold values from -0.125 to 0.125
- value_weight: bfloat16 [4, 4096, 4096], P('section', None, 'tp'), may hold values from -0.125 to 0.125
- out_weight: bfloat16 [4, 4096, 4096], P('section', 'tp'), may hold values from -0.09375 to 0.09375
Outputs:
- grad_out: bfloat16 [4, 128, 4096], P('section', None, 'tp')
- acc_out: float32 [4, 128, 4096], P('section', None, 'tp')
All inputs are finite; a program needn't handle non-finite values.
Results may differ from a plain program's by a relative error of at most 0.025.
Values may be sent and summed in bfloat16 or wider, within the bound.
A program may use at most 64 MiB of HBM per device.

v0:
```python
import jax
import jax.numpy as jnp
from jax import lax
from jax.sharding import PartitionSpec as P

HEAD_DIM = 64
SEQS = 1


def passed_along(value, axis, steps):
    count = lax.axis_size(axis)
    leading, last = (max(0, -steps), min(count, count - steps))
    return lax.ppermute(value, axis, [(source, source + steps) for source in range(leading, last)])


def transpose_product(left, right):
    return lax.dot_general(
        left, right, (((1,), (1,)), ((), ())), preferred_element_type=jnp.float32
    )


def attention_grads(upstream, queries, keys, values):
    token_rows, columns = queries.shape
    enc_rows = keys.shape[0]
    heads = columns // HEAD_DIM
    query_heads = queries.reshape(SEQS, token_rows // SEQS, heads, HEAD_DIM)
    key_heads = keys.reshape(SEQS, enc_rows // SEQS, heads, HEAD_DIM)
    value_heads = values.reshape(SEQS, enc_rows // SEQS, heads, HEAD_DIM)
    upstream_heads = upstream.reshape(SEQS, token_rows // SEQS, heads, HEAD_DIM)
    scores = jnp.einsum(
        "bqhd,bkhd->bhqk", query_heads, key_heads, preferred_element_type=jnp.float32
    )
    attention = jax.nn.softmax(scores, axis=-1)
    weights = attention.astype(jnp.bfloat16)
    output = jnp.einsum("bhqk,bkhd->bqhd", weights, value_heads, preferred_element_type=jnp.float32)
    delta = jnp.sum(upstream_heads.astype(jnp.float32) * output, axis=-1)
    prob_grad = jnp.einsum(
        "bqhd,bkhd->bhqk", upstream_heads, value_heads, preferred_element_type=jnp.float32
    )
    score_grad = (attention * (prob_grad - jnp.transpose(delta, (0, 2, 1))[..., None])).astype(
        jnp.bfloat16
    )
    query_grad = jnp.einsum(
        "bhqk,bkhd->bqhd", score_grad, key_heads, preferred_element_type=jnp.float32
    )
    key_grad = jnp.einsum(
        "bhqk,bqhd->bkhd", score_grad, query_heads, preferred_element_type=jnp.float32
    )
    value_grad = jnp.einsum(
        "bhqk,bqhd->bkhd", weights, upstream_heads, preferred_element_type=jnp.float32
    )
    return (
        query_grad.reshape(token_rows, columns).astype(jnp.bfloat16),
        key_grad.reshape(enc_rows, columns).astype(jnp.bfloat16),
        value_grad.reshape(enc_rows, columns).astype(jnp.bfloat16),
    )


def body(
    grad_in,
    fresh_grads,
    acc_in,
    queries,
    keys,
    values,
    query_weight,
    key_weight,
    value_weight,
    out_weight,
):
    grad_slice = grad_in[0]
    carried = acc_in[0]
    w_query = query_weight[0]
    w_key = key_weight[0]
    w_value = value_weight[0]
    w_out = out_weight[0]
    slot_count = queries.shape[1]
    is_top = lax.axis_index("section") == lax.axis_size("section") - 1
    passed = grad_slice
    for slot in range(slot_count):
        upstream = transpose_product(lax.all_gather(grad_slice, "tp", axis=1, tiled=True), w_out)
        query_grad, key_grad, value_grad = attention_grads(
            upstream.astype(jnp.bfloat16), queries[0, slot], keys[0, slot], values[0, slot]
        )
        branch = transpose_product(lax.all_gather(query_grad, "tp", axis=1, tiled=True), w_query)
        passed = (grad_slice.astype(jnp.float32) + branch).astype(jnp.bfloat16)
        passes_on = slot + 1 < slot_count
        summed = carried
        term = transpose_product(key_grad, w_key) + transpose_product(value_grad, w_value)
        summed = summed + lax.psum_scatter(
            term.astype(jnp.bfloat16), "tp", scatter_dimension=1, tiled=True
        ).astype(jnp.float32)
        if passes_on:
            summed = passed_along(summed.astype(jnp.bfloat16), "section", -1).astype(summed.dtype)
        carried = summed
        if passes_on:
            received = passed_along(passed, "section", -1)
            new_slice = jnp.where(is_top, fresh_grads[slot], received)
            grad_slice = new_slice
            pass
    return (passed[None], carried[None])


def solution(mesh):
    in_specs = (
        P("section", None, "tp"),
        P(None, None, "tp"),
        P("section", None, "tp"),
        P("section", None, None, "tp"),
        P("section", None, None, "tp"),
        P("section", None, None, "tp"),
        P("section", "tp", None),
        P("section", None, "tp"),
        P("section", None, "tp"),
        P("section", "tp", None),
    )
    out_specs = (P("section", None, "tp"), P("section", None, "tp"))
    return jax.shard_map(body, mesh=mesh, in_specs=in_specs, out_specs=out_specs, check_vma=False)
```

profile of v0, /device:TPU:0, one launch (start us, length us, event | category | flops | bytes accessed | tf_op | source)
XLA Modules:
  0.0 196.2 jit_solution(3689854424168437821)
XLA Ops:
  7.2 0.7 all-gather.12.cloned.1.call-update
  7.9 1.0 fusion.55
  8.9 0.1 copy.34
  9.1 1.0 fusion.57
  10.1 0.1 copy.35
  10.2 1.0 fusion.56
  11.2 0.1 copy.37
  11.3 0.4 fusion.58
  11.7 22.9 %all-gather.12.cloned.1.call-done = bf16[1,128,4096]{2,1,0:T(8,128)(2,1)} async-done(((bf16[1,128,512]{2,1,0:T(8,128)(2,1)}), bf16[1,128,4096]{2,1,0:T(8,128)(2,1)}) %all-gather.12.cloned.1.call-update) | async-done | bytes 1048592 | tf_op jit(solution)/shard_map/all_gather | solution.py:81
  34.6 4.0 %fusion.31 = bf16[128,512]{1,0:T(8,128)(2,1)S(1)} fusion(bf16[1,512,4096]{2,1,0:T(8,128)(2,1)} %param.19, bf16[1,128,4096]{2,1,0:T(8,128)(2,1)} %all-gather.12.cloned.1.call-done), kind=kOutput, calls=%fused_computation.35 | convolution fusion | flops 536936448 | bytes 5373952 | tf_op jit(solution)/shard_map/dot_general | solution.py:17
  38.6 0.1 copy.36
  38.7 0.1 copy.38
  38.9 0.2 fusion.40
  39.1 0.3 fusion.25
  39.4 0.9 convolution_convert_fusion.1
  40.3 21.9 %all-gather.6.cloned.1.call-done = bf16[128,4096]{0,1:T(8,128)(2,1)} async-done(((bf16[128,512]{0,1:T(8,128)(2,1)}), bf16[128,4096]{0,1:T(8,128)(2,1)}) %all-gather.6.cloned.1.call-update) | async-done | bytes 1048592 | tf_op jit(solution)/shard_map/all_gather | solution.py:85
  62.3 4.0 %fusion.37 = bf16[128,512]{1,0:T(8,128)(2,1)S(1)} fusion(bf16[128,4096]{0,1:T(8,128)(2,1)} %all-gather.6.cloned.1.call-done, bf16[1,512,4096]{2,1,0:T(8,128)(2,1)} %param.16, bf16[1,128,512]{2,1,0:T(8,128)(2,1)S(1)} %copy-done.3), kind=kOutput, calls=%fused_computation.43 | convolution fusion | flops 537067520 | bytes 5505024 | tf_op jit(solution)/shard_map/dot_general | solution.py:17
  66.3 1.3 collective-permute-start
  67.6 6.2 %collective-permute-done = bf16[128,512]{1,0:T(8,128)(2,1)S(1)} collective-permute-done((bf16[128,512]{1,0:T(8,128)(2,1)S(1)}, bf16[128,512]{1,0:T(8,128)(2,1)S(1)}, u32[]{:S(2)}, u32[]{:S(2)}) %collective-permute-start) | collective-permute-done | bytes 131104 | tf_op jit(solution)/shard_map/ppermute | solution.py:13
  73.8 0.7 bitcast_select_fusion
  74.5 0.0 reduce-scatter.3.cloned.1.call-start
  74.6 0.3 convolution_convert_fusion.5
  74.9 0.3 convolution_convert_fusion.4
  75.2 3.8 %fusion.8 = f32[128,4096]{1,0:T(8,128)S(1)} fusion(bf16[128,512]{0,1:T(8,128)(2,1)S(1)} %bitcast.159, bf16[1,4096,512]{2,1,0:T(8,128)(2,1)} %param.17), kind=kOutput, calls=%fused_computation.10 | convolution fusion | flops 536870912 | bytes 6422528 | tf_op jit(solution)/shard_map/dot_general | solution.py:17
  79.0 2.5 %fusion.2 = bf16[128,4096]{1,0:T(8,128)(2,1)} fusion(f32[128,4096]{1,0:T(8,128)S(1)} %fusion.8, bf16[128,512]{0,1:T(8,128)(2,1)S(1)} %bitcast.165, bf16[1,4096,512]{2,1,0:T(8,128)(2,1)S(1)} %copy-done), kind=kOutput, calls=%fused_computation.4 | convolution fusion | flops 537919488 | bytes 7471104 | tf_op jit(solution)/shard_map/dot_general | solution.py:17
  81.6 0.1 copy.42
  81.7 0.1 copy.43
  81.8 0.1 copy.45
  81.9 0.4 fusion.59
  82.3 14.2 %all-gather.8.cloned.1.call-done = bf16[128,4096]{1,0:T(8,128)(2,1)} async-done(((bf16[128,512]{1,0:T(8,128)(2,1)}), bf16[128,4096]{1,0:T(8,128)(2,1)}) %all-gather.8.cloned.1.call-update) | async-done | bytes 1048592 | tf_op jit(solution)/shard_map/all_gather | solution.py:81
  96.5 4.0 %fusion.34 = bf16[128,512]{1,0:T(8,128)(2,1)S(1)} fusion(bf16[128,4096]{1,0:T(8,128)(2,1)} %all-gather.8.cloned.1.call-done, bf16[1,512,4096]{2,1,0:T(8,128)(2,1)} %param.19), kind=kOutput, calls=%fused_computation.36 | convolution fusion | flops 536936448 | bytes 5373952 | tf_op jit(solution)/shard_map/dot_general | solution.py:17
  100.5 0.1 copy.44
  100.7 0.1 copy.46
  100.8 0.2 fusion.41
  101.0 0.3 fusion.24
  101.3 0.9 convolution_convert_fusion
  102.2 0.0 reduce-scatter.5.cloned.1.call-start
  102.2 0.3 convolution_convert_fusion.3
  102.5 0.3 convolution_convert_fusion.2
  102.8 3.9 %fusion.6 = f32[128,4096]{1,0:T(8,128)S(1)} fusion(bf16[128,512]{0,1:T(8,128)(2,1)S(1)} %bitcast.160, bf16[1,4096,512]{2,1,0:T(8,128)(2,1)} %param.17), kind=kOutput, calls=%fused_computation.8 | convolution fusion | flops 536870912 | bytes 6422528 | tf_op jit(solution)/shard_map/dot_general | solution.py:17
  106.8 2.5 %fusion.3 = bf16[128,4096]{1,0:T(8,128)(2,1)} fusion(f32[128,4096]{1,0:T(8,128)S(1)} %fusion.6, bf16[128,512]{0,1:T(8,128)(2,1)S(1)} %bitcast.166, bf16[1,4096,512]{2,1,0:T(8,128)(2,1)S(1)} %copy-done.1), kind=kOutput, calls=%fused_computation.5 | convolution fusion | flops 537919488 | bytes 7471104 | tf_op jit(solution)/shard_map/dot_general | solution.py:17
  109.3 21.6 %reduce-scatter.3.cloned.1.call-done = bf16[128,512]{1,0:T(8,128)(2,1)} async-done(((bf16[128,4096]{1,0:T(8,128)(2,1)}), bf16[128,512]{1,0:T(8,128)(2,1)}) %reduce-scatter.3.cloned.1.call-update) | async-done | bytes 131088 | tf_op jit(solution)/shard_map/reduce_scatter | solution.py:90
  130.9 0.9 fusion.43
  131.8 1.3 collective-permute-start.1
  133.1 20.2 %all-gather.10.cloned.1.call-done = bf16[128,4096]{0,1:T(8,128)(2,1)} async-done(((bf16[128,512]{0,1:T(8,128)(2,1)}), bf16[128,4096]{0,1:T(8,128)(2,1)}) %all-gather.10.cloned.1.call-update) | async-done | bytes 1048592 | tf_op jit(solution)/shard_map/all_gather | solution.py:85
  153.4 4.7 %fusion.46 = bf16[1,128,512]{2,1,0:T(8,128)(2,1)} fusion(bf16[128,512]{1,0:T(8,128)(2,1)S(1)} %copy-done.2, bf16[128,4096]{0,1:T(8,128)(2,1)} %all-gather.10.cloned.1.call-done, bf16[1,512,4096]{2,1,0:T(8,128)(2,1)} %param.16), kind=kOutput, calls=%fused_computation.55 | convolution fusion | flops 537067520 | bytes 5505024 | tf_op jit(solution)/shard_map/dot_general | solution.py:17
  158.1 29.6 %reduce-scatter.5.cloned.1.call-done = bf16[128,512]{1,0:T(8,128)(2,1)} async-done(((bf16[128,4096]{1,0:T(8,128)(2,1)}), bf16[128,512]{1,0:T(8,128)(2,1)}) %reduce-scatter.5.cloned.1.call-update) | async-done | bytes 131088 | tf_op jit(solution)/shard_map/reduce_scatter | solution.py:90
  187.7 1.6 add_bitcast_fusion
  (22 shorter events, 0.3 us)
Async XLA Ops:
  7.2 27.4 %all-gather.12.cloned.1.call-start = ((), (), s32[]{:S(2)}) async-start(), calls=%async_computation.7 | async-start | bytes 1179648 | tf_op jit(solution)/shard_map/all_gather | solution.py:81
  7.9 54.4 %all-gather.6.cloned.1.call-start = ((), (), s32[]{:S(2)}) async-start(), calls=%async_computation.2 | async-start | bytes 1179648 | tf_op jit(solution)/shard_map/all_gather | solution.py:85
  11.7 50.6 %copy-start.3 = (bf16[1,128,512]{2,1,0:T(8,128)(2,1)S(1)}, bf16[1,128,512]{2,1,0:T(8,128)(2,1)}, u32[]{:S(2)}) copy-start(bf16[1,128,512]{2,1,0:T(8,128)(2,1)} %param.10) | copy-start | bytes 393220
  39.1 34.8 %copy-start.5 = (bf16[1,128,512]{2,1,0:T(8,128)(2,1)S(1)}, bf16[1,128,512]{2,1,0:T(8,128)(2,1)}, u32[]{:S(2)}) copy-start(bf16[1,128,512]{2,1,0:T(8,128)(2,1)} %param.11) | copy-start | bytes 393220
  40.3 56.2 %all-gather.8.cloned.1.call-start = ((), (), s32[]{:S(2)}) async-start(), calls=%async_computation.3 | async-start | bytes 1179648 | tf_op jit(solution)/shard_map/all_gather | solution.py:81
  66.3 7.5 %collective-permute-start = (bf16[128,512]{1,0:T(8,128)(2,1)S(1)}, bf16[128,512]{1,0:T(8,128)(2,1)S(1)}, u32[]{:S(2)}, u32[]{:S(2)}) collective-permute-start(bf16[128,512]{1,0:T(8,128)(2,1)S(1)} %fusion.37), channel_id=1, source_target_pairs={{8,0},{16,8},{24,16},{9,1},{17,9},{25,17},{10,2},{18,10},{26,18},{... | collective-permute-start | bytes 393224 | tf_op jit(solution)/shard_map/ppermute | solution.py:13
  74.5 56.4 %reduce-scatter.3.cloned.1.call-start = ((), (), s32[]{:S(2)}) async-start(), calls=%async_computation.5 | async-start | bytes 1179648 | tf_op jit(solution)/shard_map/reduce_scatter | solution.py:90
  74.9 4.2 %copy-start = (bf16[1,4096,512]{2,1,0:T(8,128)(2,1)S(1)}, bf16[1,4096,512]{2,1,0:T(8,128)(2,1)}, u32[]{:S(2)}) copy-start(bf16[1,4096,512]{2,1,0:T(8,128)(2,1)} %param.18) | copy-start | bytes 12582916
  81.5 71.9 %all-gather.10.cloned.1.call-start = ((), (), s32[]{:S(2)}) async-start(), calls=%async_computation.4 | async-start | bytes 1179648 | tf_op jit(solution)/shard_map/all_gather | solution.py:85
  102.2 85.5 %reduce-scatter.5.cloned.1.call-start = ((), (), s32[]{:S(2)}) async-start(), calls=%async_computation.6 | async-start | bytes 1179648 | tf_op jit(solution)/shard_map/reduce_scatter | solution.py:90
  102.5 4.3 %copy-start.1 = (bf16[1,4096,512]{2,1,0:T(8,128)(2,1)S(1)}, bf16[1,4096,512]{2,1,0:T(8,128)(2,1)}, u32[]{:S(2)}) copy-start(bf16[1,4096,512]{2,1,0:T(8,128)(2,1)} %param.18) | copy-start | bytes 12582916
  106.8 24.1 %copy-start.4 = (f32[1,128,512]{2,1,0:T(8,128)S(1)}, f32[1,128,512]{2,1,0:T(8,128)}, u32[]{:S(2)}) copy-start(f32[1,128,512]{2,1,0:T(8,128)} %param.12) | copy-start | bytes 786436
  106.8 46.6 %copy-start.2 = (bf16[128,512]{1,0:T(8,128)(2,1)S(1)}, bf16[128,512]{1,0:T(8,128)(2,1)}, u32[]{:S(2)}) copy-start(bf16[128,512]{1,0:T(8,128)(2,1)} %bitcast_select_fusion) | copy-start | bytes 393220
  131.8 26.2 %collective-permute-start.1 = (bf16[128,512]{1,0:T(8,128)(2,1)S(1)}, bf16[128,512]{1,0:T(8,128)(2,1)S(1)}, u32[]{:S(2)}, u32[]{:S(2)}) collective-permute-start(bf16[128,512]{1,0:T(8,128)(2,1)S(1)} %fusion.43), channel_id=1, source_target_pairs={{8,0},{16,8},{24,16},{9,1},{17,9},{25,17},{10,2},{18,10},{26,18},{... | collective-permute-start | bytes 393224 | tf_op jit(solution)/shard_map/ppermute | solution.py:13
Sparse Core Ops, SparseCore 0:
  9.6 24.9 all-gather.11
  40.4 21.8 all-gather.5
  74.7 21.7 all-gather.7
  98.6 32.2 reduce-scatter.2
  132.9 20.4 all-gather.9
  155.5 32.1 reduce-scatter.4
where the time goes:
time: 196 us
  waiting for transfers between devices  137 us (70%)
  matrix products  34.1 us (17%)
  between operations  14.3 us (7%)
  local copies, waits for them, and re-layouts  4.18 us (2%)
  other arithmetic  3.24 us (2%)
  starting transfers between devices  2.83 us (1%)
    reduce_scatter x2, waiting for transfers between devices, body(): lax.psum_scatter(term.astype(jnp.bfloat16), 'tp', scatter_dimension=1, ti...  51.2 us
    all_gather x2, waiting for transfers between devices, body(): lax.all_gather(query_grad, 'tp', axis=1, tiled=True)  42.2 us
    all_gather x2, waiting for transfers between devices, body(): lax.all_gather(grad_slice, 'tp', axis=1, tiled=True)  37.1 us
    dot_general x8, matrix products, transpose_product(): lax.dot_general(left, right, (((1,), (1,)), ((), ())), preferred_element_...  29.5 us
    ppermute x2, waiting for transfers between devices, passed_along(): lax.ppermute(value, axis, [(source, source + steps) for source in range(l...  6.21 us
  transfers between devices with their start and end apart: 8, of which 7 were waited for; matrix products, arithmetic and copies ran while one was open for 15% of the time, Pallas kernels for 0%

commit v1 on v0

--- a/solution.py
+++ b/solution.py
@@ -1,3 +1,4 @@
+import functools
 import jax
 import jax.numpy as jnp
 from jax import lax
@@ -5,6 +6,34 @@
 
 HEAD_DIM = 64
 SEQS = 1
+
+
+def reach_trees_here(shard_in, along_axis):
+    local_out = lax.axis_size(along_axis)
+    newest = lax.axis_index(along_axis)
+    local_now, res, b_next = (local_out, newest, shard_in.shape[1])
+    history = [s * local_now if num == 1 else s for num, s in enumerate(shard_in.shape)]
+    outer = jnp.zeros(history, shard_in.dtype)
+    small = lax.dynamic_update_slice_in_dim(outer, shard_in, res * b_next, axis=1)
+    response = carry_in = shard_in
+    for q in [*range(1, local_now // 2 + 1)]:
+        response = lax.ppermute(
+            response, along_axis, [(num, (num + 1) % local_now) for num in range(local_now)]
+        )
+        small = lax.dynamic_update_slice_in_dim(
+            small, response, (res - q) % local_now * b_next, axis=1
+        )
+        if 2 * q < local_now:
+            carry_in = lax.ppermute(
+                carry_in, along_axis, [(num, (num - 1) % local_now) for num in range(local_now)]
+            )
+            small = lax.dynamic_update_slice_in_dim(
+                small, carry_in, (res + q) % local_now * b_next, axis=1
+            )
+    return small
+
+
+register_block_here = functools.partial(reach_trees_here, along_axis="tp")
 
 
 def passed_along(value, axis, steps):
@@ -78,7 +107,7 @@
     is_top = lax.axis_index("section") == lax.axis_size("section") - 1
     passed = grad_slice
     for slot in range(slot_count):
-        upstream = transpose_product(lax.all_gather(grad_slice, "tp", axis=1, tiled=True), w_out)
+        upstream = transpose_product(register_block_here(grad_slice), w_out)
         query_grad, key_grad, value_grad = attention_grads(
             upstream.astype(jnp.bfloat16), queries[0, slot], keys[0, slot], values[0, slot]
         )

time: 196 us -> 176 us (0.90)
  waiting for transfers between devices: 137 us -> 95 us
  starting transfers between devices: 2.83 us -> 25.5 us
    all_gather x2 -> x0, waiting for transfers between devices: 37.1 us -> none  [body(): lax.all_gather(grad_slice, 'tp', axis=1, tiled=True)]
    ppermute x0 -> x14, waiting for transfers between devices: none -> 31.6 us  [the longest x8 31.5 us: reach_trees_here(): lax.ppermute(response, along_axis, [(num, (num + 1) % local_now) for num...]
    ppermute x0 -> x14, starting transfers between devices: none -> 22.7 us  [the longest x6 22 us: reach_trees_here(): lax.ppermute(carry_in, along_axis, [(num, (num - 1) % local_now) for num...]
    reduce_scatter x2, waiting for transfers between devices: 51.2 us -> 29.7 us  [body(): lax.psum_scatter(term.astype(jnp.bfloat16), 'tp', scatter_dimension=1, ti...]
    all_gather x2, waiting for transfers between devices: 42.2 us -> 30 us  [body(): lax.all_gather(query_grad, 'tp', axis=1, tiled=True)]
    ppermute x2, waiting for transfers between devices: 6.21 us -> 3.65 us  [passed_along(): lax.ppermute(value, axis, [(source, source + steps) for source in range(l...]
  transfers between devices with their start and end apart: 8 -> 20, of which waited for: 7 -> 12; matrix products, arithmetic and copies ran while one was open for 15% -> 17% of each run, Pallas kernels for 0% -> 0%
where the time goes in v1:
time: 176 us; the launch traced here: 175 us
  waiting for transfers between devices  95 us (54%)
  matrix products  33.5 us (19%)
  starting transfers between devices  25.5 us (14%)
  between operations  14.2 us (8%)
  local copies, waits for them, and re-layouts  4.55 us (3%)
  other arithmetic  2.61 us (1%)
    ppermute x8, waiting for transfers between devices, reach_trees_here(): lax.ppermute(response, along_axis, [(num, (num + 1) % local_now) for num...  31.5 us
    all_gather x2, waiting for transfers between devices, body(): lax.all_gather(query_grad, 'tp', axis=1, tiled=True)  30 us
    reduce_scatter x2, waiting for transfers between devices, body(): lax.psum_scatter(term.astype(jnp.bfloat16), 'tp', scatter_dimension=1, ti...  29.7 us
    dot_general x8, matrix products, transpose_product(): lax.dot_general(left, right, (((1,), (1,)), ((), ())), preferred_element_...  28.9 us
    ppermute x6, starting transfers between devices, reach_trees_here(): lax.ppermute(carry_in, along_axis, [(num, (num - 1) % local_now) for num...  22 us
    ppermute x2, waiting for transfers between devices, passed_along(): lax.ppermute(value, axis, [(source, source + steps) for source in range(l...  3.65 us
  transfers between devices with their start and end apart: 20, of which 12 were waited for; matrix products, arithmetic and copies ran while one was open for 17% of the time, Pallas kernels for 0%

profile of v1, /device:TPU:0, one launch (start us, length us, event | category | flops | bytes accessed | tf_op | source)
XLA Modules:
  0.0 175.3 jit_solution(12595333482750577755)
XLA Ops:
  7.2 0.5 collective-permute-start
  7.8 4.1 %collective-permute-start.1 = (bf16[128,512]{1,0:T(8,128)(2,1)}, bf16[128,512]{1,0:T(8,128)(2,1)S(1)}, u32[]{:S(2)}, u32[]{:S(2)}) collective-permute-start(bf16[128,512]{1,0:T(8,128)(2,1)} %bitcast.159), channel_id=1, source_target_pairs={{0,7},{1,0},{2,1},{3,2},{4,3},{5,4},{6,5},{7,6},{8,15},{9,8},{10,9... | collective-permute-start | bytes 393224 | tf_op jit(solution)/shard_map/ppermute | solution.py:27
  11.9 1.0 fusion.54
  12.8 0.1 copy.34
  13.0 1.0 fusion.56
  14.1 1.0 fusion.55
  15.2 0.4 fusion.57
  15.8 3.5 %collective-permute-start.3 = (bf16[128,512]{1,0:T(8,128)(2,1)S(1)}, bf16[128,512]{1,0:T(8,128)(2,1)S(1)}, u32[]{:S(2)}, u32[]{:S(2)}) collective-permute-start(bf16[128,512]{1,0:T(8,128)(2,1)S(1)} %collective-permute-done.1), channel_id=1, source_target_pairs={{0,7},{1,0},{2,1},{3,2},{4,3},{5,4},{6,5},{7,6},{8,15},{9,8},{10,9... | collective-permute-start | bytes 393224 | tf_op jit(solution)/shard_map/ppermute | solution.py:27
  19.4 3.3 %collective-permute-done.2 = bf16[128,512]{1,0:T(8,128)(2,1)S(1)} collective-permute-done((bf16[128,512]{1,0:T(8,128)(2,1)S(1)}, bf16[128,512]{1,0:T(8,128)(2,1)S(1)}, u32[]{:S(2)}, u32[]{:S(2)}) %collective-permute-start.2) | collective-permute-done | bytes 131104 | tf_op jit(solution)/shard_map/ppermute | solution.py:20
  22.8 3.7 %collective-permute-start.5 = (bf16[128,512]{1,0:T(8,128)(2,1)S(1)}, bf16[128,512]{1,0:T(8,128)(2,1)S(1)}, u32[]{:S(2)}, u32[]{:S(2)}) collective-permute-start(bf16[128,512]{1,0:T(8,128)(2,1)S(1)} %collective-permute-done.3), channel_id=1, source_target_pairs={{0,7},{1,0},{2,1},{3,2},{4,3},{5,4},{6,5},{7,6},{8,15},{9,8},{10,9... | collective-permute-start | bytes 393224 | tf_op jit(solution)/shard_map/ppermute | solution.py:27
  26.5 2.7 %collective-permute-done.4 = bf16[128,512]{1,0:T(8,128)(2,1)S(1)} collective-permute-done((bf16[128,512]{1,0:T(8,128)(2,1)S(1)}, bf16[128,512]{1,0:T(8,128)(2,1)S(1)}, u32[]{:S(2)}, u32[]{:S(2)}) %collective-permute-start.4) | collective-permute-done | bytes 131104 | tf_op jit(solution)/shard_map/ppermute | solution.py:20
  29.3 6.1 %collective-permute-done.6 = bf16[128,512]{1,0:T(8,128)(2,1)S(1)} collective-permute-done((bf16[128,512]{1,0:T(8,128)(2,1)S(1)}, bf16[128,512]{1,0:T(8,128)(2,1)S(1)}, u32[]{:S(2)}, u32[]{:S(2)}) %collective-permute-start.6) | collective-permute-done | bytes 131104 | tf_op jit(solution)/shard_map/ppermute | solution.py:20
  35.4 3.8 %fusion.31 = bf16[128,512]{1,0:T(8,128)(2,1)S(1)} fusion(bf16[128,4096]{1,0:T(8,128)(2,1)S(1)} %constant_dynamic-update-slice_fusion.8, bf16[1,512,4096]{2,1,0:T(8,128)(2,1)} %param.19), kind=kOutput, calls=%fused_computation.35 | convolution fusion | flops 536936448 | bytes 5373952 | tf_op jit(solution)/shard_map/dot_general | solution.py:46
  39.4 0.2 fusion.40
  39.7 0.3 fusion.25
  40.0 0.9 convolution_convert_fusion.1
  41.0 0.1 copy.43
  41.2 0.3 convolution_convert_fusion.5
  41.4 0.3 convolution_convert_fusion.4
  41.7 3.7 %fusion.8 = f32[128,4096]{1,0:T(8,128)S(1)} fusion(bf16[128,512]{0,1:T(8,128)(2,1)S(1)} %bitcast.160, bf16[1,4096,512]{2,1,0:T(8,128)(2,1)} %param.17), kind=kOutput, calls=%fused_computation.10 | convolution fusion | flops 536870912 | bytes 6422528 | tf_op jit(solution)/shard_map/dot_general | solution.py:46
  45.4 16.5 %all-gather.3.cloned.1.call-done = bf16[128,4096]{0,1:T(8,128)(2,1)} async-done(((bf16[128,512]{0,1:T(8,128)(2,1)}), bf16[128,4096]{0,1:T(8,128)(2,1)}) %all-gather.3.cloned.1.call-update) | async-done | bytes 1048592 | tf_op jit(solution)/shard_map/all_gather | solution.py:114
  62.0 4.2 %fusion.37 = bf16[128,512]{1,0:T(8,128)(2,1)S(1)} fusion(bf16[128,4096]{0,1:T(8,128)(2,1)} %all-gather.3.cloned.1.call-done, bf16[1,512,4096]{2,1,0:T(8,128)(2,1)} %param.16, bf16[1,128,512]{2,1,0:T(8,128)(2,1)S(1)} %copy-done.2), kind=kOutput, calls=%fused_computation.43 | convolution fusion | flops 537067520 | bytes 5505024 | tf_op jit(solution)/shard_map/dot_general | solution.py:46
  66.2 1.3 collective-permute-start.7
  67.5 2.5 %fusion.2 = bf16[128,4096]{1,0:T(8,128)(2,1)} fusion(f32[128,4096]{1,0:T(8,128)S(1)} %fusion.8, bf16[128,512]{0,1:T(8,128)(2,1)S(1)} %bitcast.166, bf16[1,4096,512]{2,1,0:T(8,128)(2,1)S(1)} %copy-done), kind=kOutput, calls=%fused_computation.4 | convolution fusion | flops 537919488 | bytes 7471104 | tf_op jit(solution)/shard_map/dot_general | solution.py:46
  70.0 3.7 %collective-permute-done.7 = bf16[128,512]{1,0:T(8,128)(2,1)S(1)} collective-permute-done((bf16[128,512]{1,0:T(8,128)(2,1)S(1)}, bf16[128,512]{1,0:T(8,128)(2,1)S(1)}, u32[]{:S(2)}, u32[]{:S(2)}) %collective-permute-start.7) | collective-permute-done | bytes 131104 | tf_op jit(solution)/shard_map/ppermute | solution.py:42
  73.9 3.5 %collective-permute-start.9 = (bf16[128,512]{1,0:T(8,128)(2,1)S(1)}, bf16[128,512]{1,0:T(8,128)(2,1)S(1)}, u32[]{:S(2)}, u32[]{:S(2)}) collective-permute-start(bf16[128,512]{1,0:T(8,128)(2,1)S(1)} %get-tuple-element.3), channel_id=1, source_target_pairs={{0,7},{1,0},{2,1},{3,2},{4,3},{5,4},{6,5},{7,6},{8,15},{9,8},{10,9... | collective-permute-start | bytes 393224 | tf_op jit(solution)/shard_map/ppermute | solution.py:27
  77.4 0.4 fusion.58
  77.8 0.1 copy.45
  77.9 3.1 %collective-permute-done.8 = bf16[128,512]{1,0:T(8,128)(2,1)S(1)} collective-permute-done((bf16[128,512]{1,0:T(8,128)(2,1)S(1)}, bf16[128,512]{1,0:T(8,128)(2,1)S(1)}, u32[]{:S(2)}, u32[]{:S(2)}) %collective-permute-start.8) | collective-permute-done | bytes 131104 | tf_op jit(solution)/shard_map/ppermute | solution.py:20
  81.0 3.6 %collective-permute-start.11 = (bf16[128,512]{1,0:T(8,128)(2,1)S(1)}, bf16[128,512]{1,0:T(8,128)(2,1)S(1)}, u32[]{:S(2)}, u32[]{:S(2)}) collective-permute-start(bf16[128,512]{1,0:T(8,128)(2,1)S(1)} %collective-permute-done.9), channel_id=1, source_target_pairs={{0,7},{1,0},{2,1},{3,2},{4,3},{5,4},{6,5},{7,6},{8,15},{9,8},{10,9... | collective-permute-start | bytes 393224 | tf_op jit(solution)/shard_map/ppermute | solution.py:27
  84.6 5.2 %collective-permute-done.10 = bf16[128,512]{1,0:T(8,128)(2,1)S(1)} collective-permute-done((bf16[128,512]{1,0:T(8,128)(2,1)S(1)}, bf16[128,512]{1,0:T(8,128)(2,1)S(1)}, u32[]{:S(2)}, u32[]{:S(2)}) %collective-permute-start.10) | collective-permute-done | bytes 131104 | tf_op jit(solution)/shard_map/ppermute | solution.py:20
  89.8 3.6 %collective-permute-start.13 = (bf16[128,512]{1,0:T(8,128)(2,1)S(1)}, bf16[128,512]{1,0:T(8,128)(2,1)S(1)}, u32[]{:S(2)}, u32[]{:S(2)}) collective-permute-start(bf16[128,512]{1,0:T(8,128)(2,1)S(1)} %collective-permute-done.11), channel_id=1, source_target_pairs={{0,7},{1,0},{2,1},{3,2},{4,3},{5,4},{6,5},{7,6},{8,15},{9,8},{10,9... | collective-permute-start | bytes 393224 | tf_op jit(solution)/shard_map/ppermute | solution.py:27
  93.5 4.5 %collective-permute-done.12 = bf16[128,512]{1,0:T(8,128)(2,1)S(1)} collective-permute-done((bf16[128,512]{1,0:T(8,128)(2,1)S(1)}, bf16[128,512]{1,0:T(8,128)(2,1)S(1)}, u32[]{:S(2)}, u32[]{:S(2)}) %collective-permute-start.12) | collective-permute-done | bytes 131104 | tf_op jit(solution)/shard_map/ppermute | solution.py:20
  98.0 6.7 %collective-permute-done.14 = bf16[128,512]{1,0:T(8,128)(2,1)S(1)} collective-permute-done((bf16[128,512]{1,0:T(8,128)(2,1)S(1)}, bf16[128,512]{1,0:T(8,128)(2,1)S(1)}, u32[]{:S(2)}, u32[]{:S(2)}) %collective-permute-start.14) | collective-permute-done | bytes 131104 | tf_op jit(solution)/shard_map/ppermute | solution.py:20
  104.6 3.7 %fusion.34 = bf16[128,512]{1,0:T(8,128)(2,1)S(1)} fusion(bf16[128,4096]{1,0:T(8,128)(2,1)S(1)} %constant_dynamic-update-slice_fusion, bf16[1,512,4096]{2,1,0:T(8,128)(2,1)} %param.19), kind=kOutput, calls=%fused_computation.36 | convolution fusion | flops 536936448 | bytes 5373952 | tf_op jit(solution)/shard_map/dot_general | solution.py:46
  108.6 0.2 fusion.41
  108.9 0.3 fusion.24
  109.1 0.9 convolution_convert_fusion
  110.1 0.3 convolution_convert_fusion.3
  110.4 0.3 convolution_convert_fusion.2
  110.7 3.8 %fusion.6 = f32[128,4096]{1,0:T(8,128)S(1)} fusion(bf16[128,512]{0,1:T(8,128)(2,1)S(1)} %bitcast.161, bf16[1,4096,512]{2,1,0:T(8,128)(2,1)} %param.17), kind=kOutput, calls=%fused_computation.8 | convolution fusion | flops 536870912 | bytes 6422528 | tf_op jit(solution)/shard_map/dot_general | solution.py:46
  114.5 2.5 %fusion.3 = bf16[128,4096]{1,0:T(8,128)(2,1)} fusion(f32[128,4096]{1,0:T(8,128)S(1)} %fusion.6, bf16[128,512]{0,1:T(8,128)(2,1)S(1)} %bitcast.167, bf16[1,4096,512]{2,1,0:T(8,128)(2,1)S(1)} %copy-done.1), kind=kOutput, calls=%fused_computation.5 | convolution fusion | flops 537919488 | bytes 7471104 | tf_op jit(solution)/shard_map/dot_general | solution.py:46
  117.1 0.9 fusion.42
  118.0 1.3 collective-permute-start.15
  119.3 13.4 %all-gather.5.cloned.1.call-done = bf16[128,4096]{0,1:T(8,128)(2,1)} async-done(((bf16[128,512]{0,1:T(8,128)(2,1)}), bf16[128,4096]{0,1:T(8,128)(2,1)}) %all-gather.5.cloned.1.call-update) | async-done | bytes 1048592 | tf_op jit(solution)/shard_map/all_gather | solution.py:114
  132.8 4.7 %fusion.45 = bf16[1,128,512]{2,1,0:T(8,128)(2,1)} fusion(bf16[128,512]{1,0:T(8,128)(2,1)S(1)} %get-tuple-element.3, bf16[128,4096]{0,1:T(8,128)(2,1)} %all-gather.5.cloned.1.call-done, bf16[1,512,4096]{2,1,0:T(8,128)(2,1)} %param.16), kind=kOutput, calls=%fused_computation.54 | convolution fusion | flops 537067520 | bytes 5505024 | tf_op jit(solution)/shard_map/dot_general | solution.py:46
  137.5 29.7 %reduce-scatter.5.cloned.1.call-done = bf16[128,512]{1,0:T(8,128)(2,1)} async-done(((bf16[128,4096]{1,0:T(8,128)(2,1)}), bf16[128,512]{1,0:T(8,128)(2,1)}) %reduce-scatter.5.cloned.1.call-update) | async-done | bytes 131088 | tf_op jit(solution)/shard_map/reduce_scatter | solution.py:119
  167.1 1.6 add_bitcast_fusion
  (59 shorter events, 1.8 us)
Async XLA Ops:
  7.2 8.5 %copy-start.2 = (bf16[1,128,512]{2,1,0:T(8,128)(2,1)S(1)}, bf16[1,128,512]{2,1,0:T(8,128)(2,1)}, u32[]{:S(2)}) copy-start(bf16[1,128,512]{2,1,0:T(8,128)(2,1)} %param.10) | copy-start | bytes 393220
  7.2 54.8 %all-gather.3.cloned.1.call-start = ((), (), s32[]{:S(2)}) async-start(), calls=%async_computation.2 | async-start | bytes 1179648 | tf_op jit(solution)/shard_map/all_gather | solution.py:114
  7.2 8.5 %collective-permute-start = (bf16[128,512]{1,0:T(8,128)(2,1)}, bf16[128,512]{1,0:T(8,128)(2,1)S(1)}, u32[]{:S(2)}, u32[]{:S(2)}) collective-permute-start(bf16[128,512]{1,0:T(8,128)(2,1)} %bitcast.158), channel_id=1, source_target_pairs={{0,1},{1,2},{2,3},{3,4},{4,5},{5,6},{6,7},{7,0},{8,9},{9,10},{10,1... | collective-permute-start | bytes 393224 | tf_op jit(solution)/shard_map/ppermute | solution.py:20
  7.8 8.1 %collective-permute-start.1 = (bf16[128,512]{1,0:T(8,128)(2,1)}, bf16[128,512]{1,0:T(8,128)(2,1)S(1)}, u32[]{:S(2)}, u32[]{:S(2)}) collective-permute-start(bf16[128,512]{1,0:T(8,128)(2,1)} %bitcast.159), channel_id=1, source_target_pairs={{0,7},{1,0},{2,1},{3,2},{4,3},{5,4},{6,5},{7,6},{8,15},{9,8},{10,9... | collective-permute-start | bytes 393224 | tf_op jit(solution)/shard_map/ppermute | solution.py:27
  15.8 6.9 %collective-permute-start.2 = (bf16[128,512]{1,0:T(8,128)(2,1)S(1)}, bf16[128,512]{1,0:T(8,128)(2,1)S(1)}, u32[]{:S(2)}, u32[]{:S(2)}) collective-permute-start(bf16[128,512]{1,0:T(8,128)(2,1)S(1)} %collective-permute-done), channel_id=1, source_target_pairs={{0,1},{1,2},{2,3},{3,4},{4,5},{5,6},{6,7},{7,0},{8,9},{9,10},{10,1... | collective-permute-start | bytes 393224 | tf_op jit(solution)/shard_map/ppermute | solution.py:20
  15.8 6.9 %collective-permute-start.3 = (bf16[128,512]{1,0:T(8,128)(2,1)S(1)}, bf16[128,512]{1,0:T(8,128)(2,1)S(1)}, u32[]{:S(2)}, u32[]{:S(2)}) collective-permute-start(bf16[128,512]{1,0:T(8,128)(2,1)S(1)} %collective-permute-done.1), channel_id=1, source_target_pairs={{0,7},{1,0},{2,1},{3,2},{4,3},{5,4},{6,5},{7,6},{8,15},{9,8},{10,9... | collective-permute-start | bytes 393224 | tf_op jit(solution)/shard_map/ppermute | solution.py:27
  22.7 6.6 %collective-permute-start.4 = (bf16[128,512]{1,0:T(8,128)(2,1)S(1)}, bf16[128,512]{1,0:T(8,128)(2,1)S(1)}, u32[]{:S(2)}, u32[]{:S(2)}) collective-permute-start(bf16[128,512]{1,0:T(8,128)(2,1)S(1)} %collective-permute-done.2), channel_id=1, source_target_pairs={{0,1},{1,2},{2,3},{3,4},{4,5},{5,6},{6,7},{7,0},{8,9},{9,10},{10,1... | collective-permute-start | bytes 393224 | tf_op jit(solution)/shard_map/ppermute | solution.py:20
  22.8 6.5 %collective-permute-start.5 = (bf16[128,512]{1,0:T(8,128)(2,1)S(1)}, bf16[128,512]{1,0:T(8,128)(2,1)S(1)}, u32[]{:S(2)}, u32[]{:S(2)}) collective-permute-start(bf16[128,512]{1,0:T(8,128)(2,1)S(1)} %collective-permute-done.3), channel_id=1, source_target_pairs={{0,7},{1,0},{2,1},{3,2},{4,3},{5,4},{6,5},{7,6},{8,15},{9,8},{10,9... | collective-permute-start | bytes 393224 | tf_op jit(solution)/shard_map/ppermute | solution.py:27
  29.2 6.2 %collective-permute-start.6 = (bf16[128,512]{1,0:T(8,128)(2,1)S(1)}, bf16[128,512]{1,0:T(8,128)(2,1)S(1)}, u32[]{:S(2)}, u32[]{:S(2)}) collective-permute-start(bf16[128,512]{1,0:T(8,128)(2,1)S(1)} %collective-permute-done.4), channel_id=1, source_target_pairs={{0,1},{1,2},{2,3},{3,4},{4,5},{5,6},{6,7},{7,0},{8,9},{9,10},{10,1... | collective-permute-start | bytes 393224 | tf_op jit(solution)/shard_map/ppermute | solution.py:20
  40.9 76.2 %reduce-scatter.3.cloned.1.call-start = ((), (), s32[]{:S(2)}) async-start(), calls=%async_computation.4 | async-start | bytes 1179648 | tf_op jit(solution)/shard_map/reduce_scatter | solution.py:119
  62.0 5.5 %copy-start = (bf16[1,4096,512]{2,1,0:T(8,128)(2,1)S(1)}, bf16[1,4096,512]{2,1,0:T(8,128)(2,1)}, u32[]{:S(2)}) copy-start(bf16[1,4096,512]{2,1,0:T(8,128)(2,1)} %param.18) | copy-start | bytes 12582916
  66.2 7.5 %collective-permute-start.7 = (bf16[128,512]{1,0:T(8,128)(2,1)S(1)}, bf16[128,512]{1,0:T(8,128)(2,1)S(1)}, u32[]{:S(2)}, u32[]{:S(2)}) collective-permute-start(bf16[128,512]{1,0:T(8,128)(2,1)S(1)} %fusion.37), channel_id=1, source_target_pairs={{8,0},{16,8},{24,16},{9,1},{17,9},{25,17},{10,2},{18,10},{26,18},{... | collective-permute-start | bytes 393224 | tf_op jit(solution)/shard_map/ppermute | solution.py:42
  67.5 6.3 %copy-start.4 = (bf16[1,128,512]{2,1,0:T(8,128)(2,1)S(1)}, bf16[1,128,512]{2,1,0:T(8,128)(2,1)}, u32[]{:S(2)}) copy-start(bf16[1,128,512]{2,1,0:T(8,128)(2,1)} %param.11) | copy-start | bytes 393220
  70.0 62.8 %all-gather.5.cloned.1.call-start = ((), (), s32[]{:S(2)}) async-start(), calls=%async_computation.3 | async-start | bytes 1179648 | tf_op jit(solution)/shard_map/all_gather | solution.py:114
  73.8 7.1 %collective-permute-start.8 = (bf16[128,512]{1,0:T(8,128)(2,1)S(1)}, bf16[128,512]{1,0:T(8,128)(2,1)S(1)}, u32[]{:S(2)}, u32[]{:S(2)}) collective-permute-start(bf16[128,512]{1,0:T(8,128)(2,1)S(1)} %get-tuple-element.3), channel_id=1, source_target_pairs={{0,1},{1,2},{2,3},{3,4},{4,5},{5,6},{6,7},{7,0},{8,9},{9,10},{10,1... | collective-permute-start | bytes 393224 | tf_op jit(solution)/shard_map/ppermute | solution.py:20
  73.9 7.1 %collective-permute-start.9 = (bf16[128,512]{1,0:T(8,128)(2,1)S(1)}, bf16[128,512]{1,0:T(8,128)(2,1)S(1)}, u32[]{:S(2)}, u32[]{:S(2)}) collective-permute-start(bf16[128,512]{1,0:T(8,128)(2,1)S(1)} %get-tuple-element.3), channel_id=1, source_target_pairs={{0,7},{1,0},{2,1},{3,2},{4,3},{5,4},{6,5},{7,6},{8,15},{9,8},{10,9... | collective-permute-start | bytes 393224 | tf_op jit(solution)/shard_map/ppermute | solution.py:27
  81.0 8.8 %collective-permute-start.10 = (bf16[128,512]{1,0:T(8,128)(2,1)S(1)}, bf16[128,512]{1,0:T(8,128)(2,1)S(1)}, u32[]{:S(2)}, u32[]{:S(2)}) collective-permute-start(bf16[128,512]{1,0:T(8,128)(2,1)S(1)} %collective-permute-done.8), channel_id=1, source_target_pairs={{0,1},{1,2},{2,3},{3,4},{4,5},{5,6},{6,7},{7,0},{8,9},{9,10},{10,1... | collective-permute-start | bytes 393224 | tf_op jit(solution)/shard_map/ppermute | solution.py:20
  81.0 8.8 %collective-permute-start.11 = (bf16[128,512]{1,0:T(8,128)(2,1)S(1)}, bf16[128,512]{1,0:T(8,128)(2,1)S(1)}, u32[]{:S(2)}, u32[]{:S(2)}) collective-permute-start(bf16[128,512]{1,0:T(8,128)(2,1)S(1)} %collective-permute-done.9), channel_id=1, source_target_pairs={{0,7},{1,0},{2,1},{3,2},{4,3},{5,4},{6,5},{7,6},{8,15},{9,8},{10,9... | collective-permute-start | bytes 393224 | tf_op jit(solution)/shard_map/ppermute | solution.py:27
  89.8 8.1 %collective-permute-start.12 = (bf16[128,512]{1,0:T(8,128)(2,1)S(1)}, bf16[128,512]{1,0:T(8,128)(2,1)S(1)}, u32[]{:S(2)}, u32[]{:S(2)}) collective-permute-start(bf16[128,512]{1,0:T(8,128)(2,1)S(1)} %collective-permute-done.10), channel_id=1, source_target_pairs={{0,1},{1,2},{2,3},{3,4},{4,5},{5,6},{6,7},{7,0},{8,9},{9,10},{10,1... | collective-permute-start | bytes 393224 | tf_op jit(solution)/shard_map/ppermute | solution.py:20
  89.8 8.1 %collective-permute-start.13 = (bf16[128,512]{1,0:T(8,128)(2,1)S(1)}, bf16[128,512]{1,0:T(8,128)(2,1)S(1)}, u32[]{:S(2)}, u32[]{:S(2)}) collective-permute-start(bf16[128,512]{1,0:T(8,128)(2,1)S(1)} %collective-permute-done.11), channel_id=1, source_target_pairs={{0,7},{1,0},{2,1},{3,2},{4,3},{5,4},{6,5},{7,6},{8,15},{9,8},{10,9... | collective-permute-start | bytes 393224 | tf_op jit(solution)/shard_map/ppermute | solution.py:27
  97.9 6.7 %collective-permute-start.14 = (bf16[128,512]{1,0:T(8,128)(2,1)S(1)}, bf16[128,512]{1,0:T(8,128)(2,1)S(1)}, u32[]{:S(2)}, u32[]{:S(2)}) collective-permute-start(bf16[128,512]{1,0:T(8,128)(2,1)S(1)} %collective-permute-done.12), channel_id=1, source_target_pairs={{0,1},{1,2},{2,3},{3,4},{4,5},{5,6},{6,7},{7,0},{8,9},{9,10},{10,1... | collective-permute-start | bytes 393224 | tf_op jit(solution)/shard_map/ppermute | solution.py:20
  110.0 57.1 %reduce-scatter.5.cloned.1.call-start = ((), (), s32[]{:S(2)}) async-start(), calls=%async_computation.5 | async-start | bytes 1179648 | tf_op jit(solution)/shard_map/reduce_scatter | solution.py:119
  110.3 4.2 %copy-start.1 = (bf16[1,4096,512]{2,1,0:T(8,128)(2,1)S(1)}, bf16[1,4096,512]{2,1,0:T(8,128)(2,1)}, u32[]{:S(2)}) copy-start(bf16[1,4096,512]{2,1,0:T(8,128)(2,1)} %param.18) | copy-start | bytes 12582916
  114.5 2.6 %copy-start.3 = (f32[1,128,512]{2,1,0:T(8,128)S(1)}, f32[1,128,512]{2,1,0:T(8,128)}, u32[]{:S(2)}) copy-start(f32[1,128,512]{2,1,0:T(8,128)} %param.12) | copy-start | bytes 786436
  118.0 19.4 %collective-permute-start.15 = (bf16[128,512]{1,0:T(8,128)(2,1)S(1)}, bf16[128,512]{1,0:T(8,128)(2,1)S(1)}, u32[]{:S(2)}, u32[]{:S(2)}) collective-permute-start(bf16[128,512]{1,0:T(8,128)(2,1)S(1)} %fusion.42), channel_id=1, source_target_pairs={{8,0},{16,8},{24,16},{9,1},{17,9},{25,17},{10,2},{18,10},{26,18},{... | collective-permute-start | bytes 393224 | tf_op jit(solution)/shard_map/ppermute | solution.py:42
Sparse Core Ops, SparseCore 0:
  41.0 20.9 all-gather.2
  70.1 35.3 reduce-scatter.2
  110.2 22.5 all-gather.4
  134.9 32.2 reduce-scatter.4
